TPU v7x, 512 devices: a 8x2x16 block of a 8x8x16 slice. The times are simulated.
512 devices in a mesh: subj: 2 (over y), row: 16 (over x, core), col: 16 (over z).
Axes of the slice: x: 8, y: 2, z: 16, core: 2. Of those that a mesh axis runs over, the one named last changes fastest.
The devices are a block of a 8x8x16 slice.
Arguments:
- series: float32 [800, 65536], P(None, ('subj', 'row', 'col')), parts along dimension 1, as said below
- keep_mask: int32 [512, 256], P(('subj', 'row'), 'col'), parts along dimension 0, may hold values from 0 to 1, as said below
- row_owner: int32 [512], P('subj'), parts along dimension 0, may hold values from 0 to 15, as said below
Outputs:
- owned_tiles: bfloat16 [32, 16, 96, 128, 128], P(('subj', 'row'), 'col'), parts along dimension 0
- owned_ids: int32 [32, 16, 96], P(('subj', 'row'), 'col'), parts along dimension 0
There are 2 independent parts, one for each index of `subj`. A program takes and returns all parts, laid end to end along the dimension named above; each array names one. Nothing has to cross between parts.
Inputs may be any that keep to these rules, and one draw needn't show every extreme that they name: Each voxel's series varies over time. `keep_mask`: of the 16 tiles that one tile row has in one column block, at most 6 are kept; in every draw one owner keeps exactly 6 in each of its tile rows in some column block. `row_owner`: the 16 tile rows of a row block have 16 different owners, and every owner holds 16 tile rows, from 16 different row blocks.
All inputs are finite; a program needn't handle non-finite values.
Results may differ from a plain program's by a relative error of at most 0.0042.
Values may be sent and summed in bfloat16 or wider, within the bound.
No kernel may reach another device: no remote copies, remote signals or barrier semaphores. Data moves between devices by JAX's collectives and lax.ppermute only.
A program may use at most 64 MiB of HBM per device.

v0:
```python
import jax
import jax.numpy as jnp
from jax import lax
from jax.sharding import PartitionSpec as P

TILE = 128
epsilon = 1e-05


def compact(flat_tiles, flat_ids, capacity):
    is_valid = (flat_ids >= 0).astype(jnp.int32)
    running = jnp.cumsum(is_valid)
    slot_index = jnp.arange(capacity, dtype=jnp.int32)
    position = jnp.arange(flat_ids.shape[0], dtype=jnp.int32)
    slot_hit = (is_valid[None, :] == 1) & (running[None, :] == slot_index[:, None] + 1)
    picked = jnp.sum(jnp.where(slot_hit, position[None, :], 0), axis=1)
    present = running[-1] > slot_index
    chosen = jnp.take(flat_tiles, picked, axis=0)
    slot_tiles = jnp.where(present[:, None, None], chosen, jnp.zeros_like(chosen))
    slot_ids = jnp.where(present, jnp.take(flat_ids, picked), -1).astype(jnp.int32)
    return (slot_tiles, slot_ids)


def shards(series, keep_mask, row_owner):
    frames = series.shape[0]
    average = jnp.mean(series, axis=0, keepdims=True)
    centred = series - average
    spread = jnp.mean(centred * centred, axis=0, keepdims=True)
    scored = (centred * lax.rsqrt(spread + epsilon)).astype(jnp.bfloat16)
    row_block = lax.all_gather(scored, "col", axis=1, tiled=True)
    product = lax.dot_general(
        row_block,
        lax.all_gather(scored, "row", axis=1, tiled=True),
        (((0,), (0,)), ((), ())),
        preferred_element_type=jnp.float32,
    )
    tile_grid = (product * (1.0 / frames)).astype(jnp.bfloat16)
    row_count, col_count = keep_mask.shape
    tile_grid = tile_grid.reshape(row_count, TILE, col_count, TILE).transpose(0, 2, 1, 3)
    row_devices = lax.axis_size("row")
    col_devices = lax.axis_size("col")
    row_index = lax.axis_index("row")
    col_index = lax.axis_index("col")
    total_cols = col_count * col_devices
    slot_limit = max(2, 3 * col_count // 8)
    capacity = row_count * slot_limit
    local_owner = lax.dynamic_slice_in_dim(row_owner, row_index * row_count, row_count)
    targets = jnp.arange(row_devices, dtype=jnp.int32)
    owns_row = local_owner[None, :] == targets[:, None]
    has_row = jnp.any(owns_row, axis=1)
    row_of = jnp.sum(
        jnp.where(owns_row, jnp.arange(row_count, dtype=jnp.int32)[None, :], 0), axis=1
    )
    keep_flags = jnp.where(has_row[:, None], jnp.take(keep_mask, row_of, axis=0), 0)
    global_row = row_index * row_count + row_of
    first_col = col_index * col_count
    running = jnp.cumsum(keep_flags, axis=1)
    slot_index = jnp.arange(slot_limit, dtype=jnp.int32)
    slot_hit = (keep_flags[:, None, :] == 1) & (
        running[:, None, :] == slot_index[None, :, None] + 1
    )
    picked = jnp.sum(
        jnp.where(slot_hit, jnp.arange(col_count, dtype=jnp.int32)[None, None, :], 0), axis=2
    )
    present = running[:, -1:] > slot_index[None, :]
    chosen = tile_grid[row_of[:, None], picked]
    outgoing = jnp.where(present[:, :, None, None], chosen, jnp.zeros_like(chosen))
    out_ids = jnp.where(present, global_row[:, None] * total_cols + first_col + picked, -1)
    incoming, in_ids = (
        lax.all_to_all(outgoing, "row", split_axis=0, concat_axis=0, tiled=True),
        lax.all_to_all(out_ids, "row", split_axis=0, concat_axis=0, tiled=True),
    )
    flat_tiles = incoming.reshape(-1, TILE, TILE)
    flat_ids = in_ids.reshape(-1)
    slot_tiles, slot_ids = compact(flat_tiles, flat_ids, capacity)
    return (slot_tiles.reshape(1, 1, capacity, TILE, TILE), slot_ids.reshape(1, 1, capacity))


def solution(mesh):
    in_specs = (P(None, ("subj", "row", "col")), P(("subj", "row"), "col"), P("subj"))
    out_specs = (P(("subj", "row"), "col", None, None, None), P(("subj", "row"), "col", None))
    return jax.shard_map(shards, mesh=mesh, in_specs=in_specs, out_specs=out_specs, check_vma=False)
```

profile of v0, /device:TPU:65, one launch (start us, length us, event | category | flops | bytes accessed | tf_op | source)
XLA Modules:
  0.0 313.3 jit_solution(12894685114126903149)
XLA Ops:
  7.2 0.0 copy-start
  7.2 0.1 all-gather.3.cloned.1.call-start
  7.3 1.1 reduce_sum.60
  8.4 1.1 multiply_reduce_fusion
  9.5 1.7 multiply_convert_fusion.1
  11.3 0.1 all-gather.3.cloned.1.call-update
  11.3 0.1 all-gather.5.cloned.1.call-start
  11.4 0.7 all-gather.5.cloned.1.call-update
  12.1 0.8 dynamic_slice.3
  12.9 0.1 select_reduce_fusion.2
  13.0 0.0 copy-done
  13.0 0.6 gather_fusion
  13.6 0.1 fusion.3
  13.7 0.1 broadcast_compare_fusion
  13.8 0.2 reduce_window_sum.18
  14.0 0.2 slice_reduce_fusion
  14.2 0.3 select_reduce_fusion.1
  14.4 0.7 copy.18
  15.1 44.6 %all-to-all-start = ((s32[16,1,6]{2,1,0:T(1,128)}), s32[16,1,6]{2,1,0:T(1,128)S(1)}, u32[]{:S(2)}, u32[]{:S(2)}) async-start(s32[16,1,6]{2,1,0:T(1,128)} %copy.18), calls=%async_computation | async-start | bytes 16384 | tf_op jit(solution)/shard_map/all_to_all | solution.py:71
  59.8 0.1 copy.21
  59.9 0.1 reshape.311
  59.9 0.1 iota_compare_fusion
  60.0 64.0 %all-gather.3.cloned.1.call-done = bf16[800,2048]{1,0:T(8,128)(2,1)} async-done(((bf16[800,128]{1,0:T(8,128)(2,1)}), bf16[800,2048]{1,0:T(8,128)(2,1)}) %all-gather.3.cloned.1.call-update) | async-done | bytes 3276816 | tf_op jit(solution)/shard_map/all_gather | solution.py:30
  124.0 61.5 %all-gather.5.cloned.1.call-done = bf16[800,2048]{1,0:T(8,128)(2,1)} async-done(((bf16[800,128]{1,0:T(8,128)(2,1)}), bf16[800,2048]{1,0:T(8,128)(2,1)}) %all-gather.5.cloned.1.call-update) | async-done | bytes 3276816 | tf_op jit(solution)/shard_map/all_gather | solution.py:33
  185.5 13.6 %fusion = bf16[256,8,16,128]{3,1,2,0:T(8,128)(2,1)} fusion(bf16[800,2048]{1,0:T(8,128)(2,1)} %all-gather.3.cloned.1.call-done, bf16[800,2048]{1,0:T(8,128)(2,1)} %all-gather.5.cloned.1.call-done), kind=kOutput, calls=%fused_computation.6 | convolution fusion | flops 6719275008 | bytes 14942208 | tf_op jit(solution)/shard_map/dot_general | solution.py:31
  199.2 9.7 %copy.22 = bf16[256,8,16,128]{3,2,1,0:T(8,128)(2,1)} copy(bf16[256,8,16,128]{3,1,2,0:T(8,128)(2,1)} %fusion) | data formatting | bytes 16777216
  208.9 9.1 %copy.24 = bf16[16,128,16,128]{3,1,2,0:T(8,128)(2,1)} copy(bf16[16,128,16,128]{3,2,1,0:T(8,128)(2,1)} %bitcast.36) | data formatting | bytes 16777216 | tf_op jit(solution)/shard_map/reshape | solution.py:39
  218.0 4.9 %gather_fusion.1 = bf16[96,128,128]{2,1,0:T(8,128)(2,1)S(1)} fusion(bf16[16,16,128,128]{3,2,1,0:T(8,128)(2,1)} %bitcast.37, s32[96]{0:T(128)S(1)} %reshape.311), kind=kCustom, calls=%fused_computation.1 | custom fusion | bytes 6292224 | tf_op jit(solution)/shard_map/gather | solution.py:66
  223.0 1.9 broadcast_select_fusion
  224.9 0.0 all-to-all-done
  224.9 4.5 %all-to-all-start.1 = ((bf16[16,6,128,128]{3,2,1,0:T(8,128)(2,1)}), bf16[16,6,128,128]{3,2,1,0:T(8,128)(2,1)S(1)}, u32[]{:S(2)}, u32[]{:S(2)}) async-start(bf16[16,6,128,128]{3,2,1,0:T(8,128)(2,1)} %broadcast_select_fusion), calls=%async_computation.1 | async-start | bytes 6291456 | tf_op jit(solution)/shard_map/all_to_all | solution.py:70
  229.4 0.5 broadcast.364
  229.9 0.7 fusion.11
  230.6 0.1 reshape.333
  230.7 0.1 reduce-window.4
  230.8 0.1 reduce.3
  230.9 0.6 slice.21
  231.5 0.1 reshape.299
  231.6 0.2 select_reduce_fusion
  231.8 1.2 gather_fusion.3
  233.1 0.7 compare_and_fusion
  233.8 1.2 compare_select_fusion.6
  235.0 65.3 %all-to-all-done.1 = bf16[16,6,128,128]{3,2,1,0:T(8,128)(2,1)S(1)} async-done(((bf16[16,6,128,128]{3,2,1,0:T(8,128)(2,1)}), bf16[16,6,128,128]{3,2,1,0:T(8,128)(2,1)S(1)}, u32[]{:S(2)}, u32[]{:S(2)}) %all-to-all-start.1) | async-done | bytes 3145760 | tf_op jit(solution)/shard_map/all_to_all | solution.py:70
  300.3 2.7 gather_fusion.2
  303.0 3.4 %fusion.1 = bf16[1,1,96,128,128]{4,3,2,1,0:T(8,128)(2,1)} fusion(bf16[96,128,128]{2,1,0:T(8,128)(2,1)} %gather_fusion.2, pred[96]{0:T(512)(128)(4,1)S(1)} %get-tuple-element.8, pred[96]{0:T(512)(128)(4,1)S(1)} %get-tuple-element.9), kind=kLoop, calls=%fused_computation.8 | loop fusion | flops 3145728 | bytes 6291648 | tf_op jit(solution)/shard_map/jit(_where)/select_n | solution.py:19
  (13 shorter events, 0.1 us)
Async XLA Ops:
  7.2 5.9 %copy-start = (s32[16,16]{1,0:T(8,128)S(1)}, s32[16,16]{1,0:T(8,128)}, u32[]{:S(2)}) copy-start(s32[16,16]{1,0:T(8,128)} %param.4) | copy-start | bytes 3076
  7.2 116.8 %all-gather.3.cloned.1.call-start = ((), (), s32[]{:S(2)}) async-start(), calls=%async_computation.2 | async-start | bytes 3481600 | tf_op jit(solution)/shard_map/all_gather | solution.py:30
  11.3 174.2 %all-gather.5.cloned.1.call-start = ((), (), s32[]{:S(2)}) async-start(), calls=%async_computation.3 | async-start | bytes 3481600 | tf_op jit(solution)/shard_map/all_gather | solution.py:33
  15.1 209.8 %all-to-all-start = ((s32[16,1,6]{2,1,0:T(1,128)}), s32[16,1,6]{2,1,0:T(1,128)S(1)}, u32[]{:S(2)}, u32[]{:S(2)}) async-start(s32[16,1,6]{2,1,0:T(1,128)} %copy.18), calls=%async_computation | async-start | bytes 16384 | tf_op jit(solution)/shard_map/all_to_all | solution.py:71
  224.9 75.4 %all-to-all-start.1 = ((bf16[16,6,128,128]{3,2,1,0:T(8,128)(2,1)}), bf16[16,6,128,128]{3,2,1,0:T(8,128)(2,1)S(1)}, u32[]{:S(2)}, u32[]{:S(2)}) async-start(bf16[16,6,128,128]{3,2,1,0:T(8,128)(2,1)} %broadcast_select_fusion), calls=%async_computation.1 | async-start | bytes 6291456 | tf_op jit(solution)/shard_map/all_to_all | solution.py:70
Sparse Core Ops, SparseCore 0:
  11.4 112.5 all-gather.2
  126.6 58.8 all-gather.4
where the time goes:
time: 314 us; the launch traced here: 313 us
  waiting for transfers between devices  192 us (61%)
  starting transfers between devices  49.2 us (16%)
  local copies, waits for them, and re-layouts  31.4 us (10%)
  between operations  14.2 us (5%)
  matrix products  13.6 us (4%)
  other arithmetic  13.2 us (4%)
    all_to_all x1, waiting for transfers between devices, shards(): lax.all_to_all(outgoing, 'row', split_axis=0, concat_axis=0, tiled=True)  65.3 us
    all_gather x1, waiting for transfers between devices, shards(): row_block = lax.all_gather(scored, 'col', axis=1, tiled=True)  64 us
    all_gather x1, waiting for transfers between devices, shards(): lax.all_gather(scored, 'row', axis=1, tiled=True)  61.5 us
    all_to_all x1, starting transfers between devices, shards(): lax.all_to_all(out_ids, 'row', split_axis=0, concat_axis=0, tiled=True)  44.6 us
    dot_general x1, matrix products, shards(): lax.dot_general(row_block, lax.all_gather(scored, 'row', axis=1, tiled=Tr...  13.6 us
    unnamed x3, local copies, waits for them, and re-layouts  9.76 us
    reshape x1, local copies, waits for them, and re-layouts, shards(): tile_grid.reshape(row_count, TILE, col_count, TILE).transpose(0, 2, 1, 3)  9.11 us
  transfers between devices with their start and end apart: 4, of which 3 were waited for; matrix products, arithmetic and copies ran while one was open for 15% of the time, Pallas kernels for 0%

commit v1 on v0

--- a/solution.py
+++ b/solution.py
@@ -27,7 +27,8 @@
     centred = series - average
     spread = jnp.mean(centred * centred, axis=0, keepdims=True)
     scored = (centred * lax.rsqrt(spread + epsilon)).astype(jnp.bfloat16)
-    row_block = lax.all_gather(scored, "col", axis=1, tiled=True)
+    clean = lax.all_to_all(jnp.stack([scored] * lax.axis_size("col"), axis=0), "col", 0, 0)
+    row_block = jnp.concatenate(clean, 1)
     product = lax.dot_general(
         row_block,
         lax.all_gather(scored, "row", axis=1, tiled=True),

time: 314 us -> 340 us (1.083)
  waiting for transfers between devices: 192 us -> 205 us
  starting transfers between devices: 49.2 us -> 61.8 us
    all_to_all x0 -> x1, waiting for transfers between devices: none -> 139 us  [shards(): lax.all_to_all(jnp.stack([scored] * lax.axis_size('col'), axis=0), 'col',...]
    all_gather x1 -> x0, waiting for transfers between devices: 64 us -> none  [shards(): row_block = lax.all_gather(scored, 'col', axis=1, tiled=True)]
    all_gather x1, waiting for transfers between devices: 61.5 us -> 0.02 us  [shards(): lax.all_gather(scored, 'row', axis=1, tiled=True)]
    all_to_all x0 -> x1, starting transfers between devices: none -> 44.4 us  [shards(): lax.all_to_all(jnp.stack([scored] * lax.axis_size('col'), axis=0), 'col',...]
    all_to_all x1, starting transfers between devices: 44.6 us -> 10.1 us  [shards(): lax.all_to_all(out_ids, 'row', split_axis=0, concat_axis=0, tiled=True)]
    unnamed x3 -> x7, local copies, waits for them, and re-layouts: 9.76 us -> 9.77 us
  transfers between devices with their start and end apart: 4 -> 4, of which waited for: 3 -> 2; matrix products, arithmetic and copies ran while one was open for 15% -> 14% of each run, Pallas kernels for 0% -> 0%
where the time goes in v1:
time: 340 us; the launch traced here: 339 us
  waiting for transfers between devices  205 us (60%)
  starting transfers between devices  61.8 us (18%)
  local copies, waits for them, and re-layouts  32.8 us (10%)
  between operations  14.2 us (4%)
  matrix products  13.1 us (4%)
  other arithmetic  12.6 us (4%)
    all_to_all x1, waiting for transfers between devices, shards(): lax.all_to_all(jnp.stack([scored] * lax.axis_size('col'), axis=0), 'col',...  139 us
    all_to_all x1, waiting for transfers between devices, shards(): lax.all_to_all(outgoing, 'row', split_axis=0, concat_axis=0, tiled=True)  65.3 us
    all_to_all x1, starting transfers between devices, shards(): lax.all_to_all(jnp.stack([scored] * lax.axis_size('col'), axis=0), 'col',...  44.4 us
    dot_general x1, matrix products, shards(): lax.dot_general(row_block, lax.all_gather(scored, 'row', axis=1, tiled=Tr...  13.1 us
    all_to_all x1, starting transfers between devices, shards(): lax.all_to_all(out_ids, 'row', split_axis=0, concat_axis=0, tiled=True)  10.1 us
    unnamed x7, local copies, waits for them, and re-layouts  9.77 us
    reshape x1, local copies, waits for them, and re-layouts, shards(): tile_grid.reshape(row_count, TILE, col_count, TILE).transpose(0, 2, 1, 3)  9.11 us
    all_to_all x1, starting transfers between devices, shards(): lax.all_to_all(outgoing, 'row', split_axis=0, concat_axis=0, tiled=True)  7.24 us
  transfers between devices with their start and end apart: 4, of which 2 were waited for; matrix products, arithmetic and copies ran while one was open for 14% of the time, Pallas kernels for 0%

profile of v1, /device:TPU:65, one launch (start us, length us, event | category | flops | bytes accessed | tf_op | source)
XLA Modules:
  0.0 339.5 jit_solution(17543250560020015228)
XLA Ops:
  7.2 0.0 copy-start
  7.2 1.1 reduce_sum.60
  8.3 1.1 multiply_reduce_fusion
  9.5 1.1 multiply_convert_fusion.1
  10.5 0.0 copy-start.1
  10.5 2.1 stack.2
  12.6 0.0 copy-done.1
  12.6 44.4 %all-to-all-start.1 = ((bf16[16,800,128]{2,1,0:T(8,128)(2,1)}), bf16[16,800,128]{2,1,0:T(8,128)(2,1)S(1)}, u32[]{:S(2)}, u32[]{:S(2)}) async-start(bf16[16,800,128]{2,1,0:T(8,128)(2,1)} %stack.2), calls=%async_computation.1 | async-start | bytes 6553600 | tf_op jit(solution)/shard_map/all_to_all | solution.py:30
  57.0 0.1 all-gather.2.cloned.1.call-start
  57.1 0.7 all-gather.2.cloned.1.call-update
  57.8 0.0 copy-done.2
  57.8 0.1 dynamic_slice.3
  57.9 0.1 select_reduce_fusion.2
  58.0 0.0 copy-done
  58.0 0.6 gather_fusion
  58.6 0.1 fusion.5
  58.7 0.1 broadcast_compare_fusion
  58.8 0.2 reduce_window_sum.18
  59.0 0.3 select_reduce_fusion.1
  59.3 0.1 copy.23
  59.3 0.1 reshape.321
  59.4 0.2 slice_reduce_fusion
  59.6 0.7 copy.19
  60.3 0.1 iota_compare_fusion
  60.4 138.9 %all-to-all-done.1 = bf16[16,800,128]{2,1,0:T(8,128)(2,1)S(1)} async-done(((bf16[16,800,128]{2,1,0:T(8,128)(2,1)}), bf16[16,800,128]{2,1,0:T(8,128)(2,1)S(1)}, u32[]{:S(2)}, u32[]{:S(2)}) %all-to-all-start.1) | async-done | bytes 3276832 | tf_op jit(solution)/shard_map/all_to_all | solution.py:30
  199.3 10.1 %all-to-all-start = ((s32[16,1,6]{2,1,0:T(1,128)}), s32[16,1,6]{2,1,0:T(1,128)S(1)}, u32[]{:S(2)}, u32[]{:S(2)}) async-start(s32[16,1,6]{2,1,0:T(1,128)} %copy.19), calls=%async_computation | async-start | bytes 16384 | tf_op jit(solution)/shard_map/all_to_all | solution.py:72
  209.4 0.0 all-gather.2.cloned.1.call-done
  209.5 13.1 %fusion = bf16[256,8,16,128]{3,1,2,0:T(8,128)(2,1)} fusion(bf16[800,2048]{1,0:T(8,128)(2,1)} %all-gather.2.cloned.1.call-done, bf16[16,800,128]{2,1,0:T(8,128)(2,1)S(1)} %all-to-all-done.1), kind=kOutput, calls=%fused_computation.6 | convolution fusion | flops 6719275008 | bytes 14942208 | tf_op jit(solution)/shard_map/dot_general | solution.py:32
  222.5 9.7 %copy.25 = bf16[256,8,16,128]{3,2,1,0:T(8,128)(2,1)} copy(bf16[256,8,16,128]{3,1,2,0:T(8,128)(2,1)} %fusion) | data formatting | bytes 16777216
  232.3 9.1 %copy.31 = bf16[16,128,16,128]{3,1,2,0:T(8,128)(2,1)} copy(bf16[16,128,16,128]{3,2,1,0:T(8,128)(2,1)} %bitcast.43) | data formatting | bytes 16777216 | tf_op jit(solution)/shard_map/reshape | solution.py:40
  241.4 4.9 %gather_fusion.1 = bf16[96,128,128]{2,1,0:T(8,128)(2,1)S(1)} fusion(bf16[16,16,128,128]{3,2,1,0:T(8,128)(2,1)} %bitcast.44, s32[96]{0:T(128)S(1)} %reshape.321), kind=kCustom, calls=%fused_computation.1 | custom fusion | bytes 6292224 | tf_op jit(solution)/shard_map/gather | solution.py:67
  246.3 1.9 broadcast_select_fusion
  248.3 0.0 all-to-all-done
  248.3 7.2 %all-to-all-start.2 = ((bf16[16,6,128,128]{3,2,1,0:T(8,128)(2,1)}), bf16[16,6,128,128]{3,2,1,0:T(8,128)(2,1)S(1)}, u32[]{:S(2)}, u32[]{:S(2)}) async-start(bf16[16,6,128,128]{3,2,1,0:T(8,128)(2,1)} %broadcast_select_fusion), calls=%async_computation.2 | async-start | bytes 6291456 | tf_op jit(solution)/shard_map/all_to_all | solution.py:71
  255.5 0.5 broadcast.366
  256.0 0.7 fusion.13
  256.7 0.1 reshape.343
  256.8 0.1 reduce-window.4
  257.0 0.1 reduce.3
  257.1 0.6 slice.21
  257.7 0.1 reshape.307
  257.8 0.2 select_reduce_fusion
  258.0 1.2 gather_fusion.3
  259.2 0.7 compare_and_fusion
  259.9 1.2 compare_select_fusion.6
  261.1 65.3 %all-to-all-done.2 = bf16[16,6,128,128]{3,2,1,0:T(8,128)(2,1)S(1)} async-done(((bf16[16,6,128,128]{3,2,1,0:T(8,128)(2,1)}), bf16[16,6,128,128]{3,2,1,0:T(8,128)(2,1)S(1)}, u32[]{:S(2)}, u32[]{:S(2)}) %all-to-all-start.2) | async-done | bytes 3145760 | tf_op jit(solution)/shard_map/all_to_all | solution.py:71
  326.5 2.7 gather_fusion.2
  329.2 3.4 %fusion.3 = bf16[1,1,96,128,128]{4,3,2,1,0:T(8,128)(2,1)} fusion(bf16[96,128,128]{2,1,0:T(8,128)(2,1)} %gather_fusion.2, pred[96]{0:T(512)(128)(4,1)S(1)} %get-tuple-element.8, pred[96]{0:T(512)(128)(4,1)S(1)} %get-tuple-element.9), kind=kLoop, calls=%fused_computation.10 | loop fusion | flops 3145728 | bytes 6291648 | tf_op jit(solution)/shard_map/jit(_where)/select_n | solution.py:19
  (14 shorter events, 0.1 us)
Async XLA Ops:
  7.2 50.9 %copy-start = (s32[16,16]{1,0:T(8,128)S(1)}, s32[16,16]{1,0:T(8,128)}, u32[]{:S(2)}) copy-start(s32[16,16]{1,0:T(8,128)} %param.4) | copy-start | bytes 3076
  10.5 2.1 copy-start.1
  12.6 45.2 %copy-start.2 = (s32[256]{0:T(256)S(1)}, s32[256]{0:T(256)}, u32[]{:S(2)}) copy-start(s32[256]{0:T(256)} %param.5) | copy-start | bytes 3076
  12.6 186.7 %all-to-all-start.1 = ((bf16[16,800,128]{2,1,0:T(8,128)(2,1)}), bf16[16,800,128]{2,1,0:T(8,128)(2,1)S(1)}, u32[]{:S(2)}, u32[]{:S(2)}) async-start(bf16[16,800,128]{2,1,0:T(8,128)(2,1)} %stack.2), calls=%async_computation.1 | async-start | bytes 6553600 | tf_op jit(solution)/shard_map/all_to_all | solution.py:30
  57.0 152.5 %all-gather.2.cloned.1.call-start = ((), (), s32[]{:S(2)}) async-start(), calls=%async_computation.3 | async-start | bytes 3481600 | tf_op jit(solution)/shard_map/all_gather | solution.py:34
  199.3 49.0 %all-to-all-start = ((s32[16,1,6]{2,1,0:T(1,128)}), s32[16,1,6]{2,1,0:T(1,128)S(1)}, u32[]{:S(2)}, u32[]{:S(2)}) async-start(s32[16,1,6]{2,1,0:T(1,128)} %copy.19), calls=%async_computation | async-start | bytes 16384 | tf_op jit(solution)/shard_map/all_to_all | solution.py:72
  248.3 78.2 %all-to-all-start.2 = ((bf16[16,6,128,128]{3,2,1,0:T(8,128)(2,1)}), bf16[16,6,128,128]{3,2,1,0:T(8,128)(2,1)S(1)}, u32[]{:S(2)}, u32[]{:S(2)}) async-start(bf16[16,6,128,128]{3,2,1,0:T(8,128)(2,1)} %broadcast_select_fusion), calls=%async_computation.2 | async-start | bytes 6291456 | tf_op jit(solution)/shard_map/all_to_all | solution.py:71
Sparse Core Ops, SparseCore 0:
  60.5 54.4 all-gather.1
